TPU v7x, 512 devices: a whole 4x8x8 slice. The times are simulated.
512 devices in a mesh: elem: 32 (over z, x), lev: 16 (over y, core).
Axes of the slice: x: 4, y: 8, z: 8, core: 2. Of those that a mesh axis runs over, the one named last changes fastest.
Arguments:
- cloud_state: float32 [4096, 8, 4096], P(('elem', 'lev')), may hold values from -6 to 6
- substeps: int32 [4096], P('elem'), may hold values from 4 to 16
- element_links: int32 [1024, 4], P('elem'), may hold values from 0 to 1023, as said below
- host_state: float32 [4, 64, 16384], P(None, 'lev', 'elem'), may hold values from -6 to 6
- wind_field: float32 [2, 64, 16384], P(None, 'lev', 'elem'), may hold values from -3 to 3
- node_mass: float32 [16384], P('elem'), may hold values from 0.25 to 4
- field_coupling: float32 [8, 8], replicated, may hold values from -2 to 2
- force_map: float32 [8, 4], replicated, may hold values from -3 to 3
- feedback_map: float32 [4, 8], replicated, may hold values from -5 to 5
Outputs:
- cloud_new: float32 [4096, 8, 4096], P(('elem', 'lev'))
- host_new: float32 [4, 64, 16384], P(None, 'lev', 'elem')
Inputs may be any that keep to these rules, and one draw needn't show every extreme that they name: `element_links`: the 1024 elements form a doubly periodic grid of 16 rows in which each index of elem holds two neighbouring grid columns, all rows, in some order; element e lies on index e // 32 of elem. Entries 0 to 3 of row e give the global index of the element to the left, right, below and above element e. An element's right edge meets its right neighbour's left edge node for node (same j), its upper edge its upper neighbour's lower edge (same i). The left neighbour lies on the same index of elem or the one before it (cyclically), the right one on the same or the one after it, the lower and upper ones on the same index.
All inputs are finite; a program needn't handle non-finite values.
Results may differ from a plain program's by a relative error of at most 0.0003.
Values sent between devices are 32-bit elements; how exact they have to be, the bound alone decides.
No kernel may reach another device: no remote copies, remote signals or barrier semaphores. Data moves between devices by JAX's collectives and lax.ppermute only.
A program may use at most 64 MiB of HBM per device.

v0:
```python
import jax
import jax.numpy as jnp
import numpy as np
from jax import lax
from jax.sharding import PartitionSpec as P

CRM_X = 64
lateral_mix = 0.2
vertical_mix = 0.2
cloud_step = 0.1
host_step = 0.1
host_mix = 0.2
highest = lax.Precision.HIGHEST


def padded_2(cells, sides, width, closed):
    for axis, dim in sides:
        count = lax.axis_size(axis)
        ends = count if closed else count - 1
        head = lax.slice_in_dim(cells, 0, width, axis=dim)
        tail = lax.slice_in_dim(cells, cells.shape[dim] - width, cells.shape[dim], axis=dim)
        cells = jnp.concatenate(
            [
                lax.ppermute(tail, axis, [(i, (i + 1) % count) for i in range(ends)]),
                cells,
                lax.ppermute(head, axis, [((i + 1) % count, i) for i in range(ends)]),
            ],
            axis=dim,
        )
    return cells


def gll_derivative():
    points = np.array([-1.0, -1.0 / np.sqrt(5.0), 1.0 / np.sqrt(5.0), 1.0])
    weights = np.array(
        [
            1.0 / np.prod([points[index] - points[other] for other in range(4) if other != index])
            for index in range(4)
        ]
    )
    matrix = np.zeros((4, 4))
    for target in range(4):
        for source in range(4):
            if target != source:
                matrix[target, source] = (
                    weights[source] / weights[target] / (points[target] - points[source])
                )
        matrix[target, target] = -np.sum(matrix[target])
    return matrix


def advance_clouds(cloud, driving, counts, coupling):
    n_rows, n_fields, n_cells = cloud.shape
    cell_width = CRM_X
    n_levels = n_cells // cell_width
    spread = jnp.repeat(driving, cell_width, axis=2)

    def one_step(stepno, current):
        extended = jnp.pad(current, ((0, 0), (0, 0), (cell_width, cell_width)))
        upper_cells = extended[:, :, 2 * cell_width :]
        lower_cells = extended[:, :, : -2 * cell_width]
        shaped = current.reshape(n_rows, n_fields, n_levels, cell_width)
        eastward = jnp.roll(shaped, -1, axis=3).reshape(current.shape)
        westward = jnp.roll(shaped, 1, axis=3).reshape(current.shape)
        reaction = jnp.tanh(jnp.einsum("gf,nfc->ngc", coupling, current, precision=highest))
        update = (
            current
            + (
                lateral_mix * (eastward + westward - 2.0 * current)
                + vertical_mix * (upper_cells + lower_cells - 2.0 * current)
            )
            + cloud_step * (reaction + spread)
        )
        return jnp.where((stepno < counts)[:, None, None], update, current)

    return lax.fori_loop(0, jnp.max(counts), one_step, cloud)


def edge_tables(element_links, n_nodes):
    elem_dev = n_nodes // 16
    quarter = 4 * elem_dev
    my_index = lax.axis_index("elem")
    node_ids = jnp.arange(n_nodes, dtype=jnp.int32)
    elem_of = node_ids // 16
    row_of = node_ids // 4 % 4
    col_of = node_ids % 4
    edge_ids = jnp.arange(2 * quarter, dtype=jnp.int32)
    inner = edge_ids % quarter
    edge_node = inner // 4 * 16 + inner % 4 * 4 + jnp.where(edge_ids < quarter, 0, 3)
    picker = (node_ids[:, None] == edge_node[None, :]).astype(jnp.float32)
    left_ids = element_links[:, 0][elem_of]
    right_ids = element_links[:, 1][elem_of]
    left_base = jnp.where(left_ids // elem_dev == my_index, 2 * quarter, 0)
    right_base = jnp.where(right_ids // elem_dev == my_index, 2 * quarter, 4 * quarter)
    left_source = left_base + quarter + left_ids % elem_dev * 4 + row_of
    right_source = right_base + right_ids % elem_dev * 4 + row_of
    side_source = jnp.where(col_of == 0, left_source, jnp.where(col_of == 3, right_source, -1))
    sideways = (jnp.arange(6 * quarter, dtype=jnp.int32)[:, None] == side_source[None, :]).astype(
        jnp.float32
    )
    lower_ids = element_links[:, 2][elem_of] % elem_dev
    upper_ids = element_links[:, 3][elem_of] % elem_dev
    lower_source = lower_ids * 16 + 12 + col_of
    upper_source = upper_ids * 16 + col_of
    vert_source = jnp.where(row_of == 0, lower_source, jnp.where(row_of == 3, upper_source, -1))
    vertical = (node_ids[:, None] == vert_source[None, :]).astype(jnp.float32)
    return (picker, sideways, vertical)


def edge_sum(quantity, tables):
    picker, sideways, vertical = tables
    lead, levels, n_nodes = quantity.shape
    flat = quantity.reshape(lead * levels, n_nodes)
    edges = jnp.dot(flat, picker, precision=highest).reshape(lead, levels, picker.shape[1])
    with_peers = padded_2(edges, (("elem", 2),), picker.shape[1], True)
    first = flat + jnp.dot(
        with_peers.reshape(lead * levels, sideways.shape[0]), sideways, precision=highest
    )
    second = first + jnp.dot(first, vertical, precision=highest)
    return second.reshape(lead, levels, n_nodes)


def shards(
    cloud_state,
    substeps,
    element_links,
    host_state,
    wind_field,
    node_mass,
    field_coupling,
    force_map,
    feedback_map,
):
    own_rows, n_fields, n_cells = cloud_state.shape
    n_vars, lev_dev, n_nodes = host_state.shape
    n_cols = substeps.shape[0]
    elem_dev = n_nodes // 16
    cell_width = CRM_X
    lev_at = lax.axis_index("lev")
    node_ids = jnp.arange(n_nodes)
    column_of_node = node_ids // 16 * 4 + node_ids // 4 % 4 // 2 * 2 + node_ids % 4 // 2
    member = (column_of_node[:, None] == jnp.arange(n_cols)[None, :]).astype(jnp.float32)
    pooling = 0.25 * member
    host_flat = host_state.reshape(n_vars * lev_dev, n_nodes)
    host_columns = (
        jnp.dot(host_flat, pooling, precision=highest)
        .reshape(n_vars, lev_dev, n_cols)
        .transpose(2, 0, 1)
    )
    every_host = lax.all_gather(host_columns, "lev", axis=2, tiled=True)
    whole_host = lax.dynamic_slice_in_dim(every_host, lev_at * own_rows, own_rows, 0)
    driving = jnp.einsum("fv,nvl->nfl", force_map, whole_host, precision=highest)
    own_counts = lax.dynamic_slice_in_dim(substeps, lev_at * own_rows, own_rows, 0)
    cloud_new = advance_clouds(cloud_state, driving, own_counts, field_coupling)
    n_levels = n_cells // cell_width
    change = (
        (cloud_new - cloud_state).reshape(own_rows, n_fields, n_levels, cell_width).mean(axis=3)
    )
    every_change = lax.all_gather(change, "lev", axis=0, tiled=True)
    level_change = lax.dynamic_slice_in_dim(every_change, lev_at * lev_dev, lev_dev, 2)
    column_tendency = jnp.einsum("vf,nfl->vln", feedback_map, level_change, precision=highest)
    physics = jnp.dot(
        column_tendency.reshape(n_vars * lev_dev, n_cols), member.T, precision=highest
    ).reshape(n_vars, lev_dev, n_nodes)
    derivative = gll_derivative()
    kron_x = jnp.asarray(np.kron(np.eye(elem_dev * 4), derivative).T, jnp.float32)
    kron_y = jnp.asarray(np.kron(np.eye(elem_dev), np.kron(derivative, np.eye(4))).T, jnp.float32)

    def tendency(field):
        flat = field.reshape(n_vars * lev_dev, n_nodes)
        along_x = jnp.dot(flat, kron_x, precision=highest).reshape(field.shape)
        along_y = jnp.dot(flat, kron_y, precision=highest).reshape(field.shape)
        padded = padded_2(field, (("lev", 1),), 1, False)
        return (
            -(wind_field[0] * along_x + wind_field[1] * along_y)
            + host_mix * (padded[:, 2:] + padded[:, :-2] - 2.0 * field)
            + physics
        )

    tables = edge_tables(element_links, n_nodes)
    mass_total = edge_sum(node_mass.reshape(1, 1, n_nodes), tables)

    def smooth(values):
        return edge_sum(node_mass * values, tables) / mass_total

    first_section = smooth(host_state + host_step * tendency(host_state))
    second_section = smooth(
        0.75 * host_state + 0.25 * (first_section + host_step * tendency(first_section))
    )
    host_new = smooth(
        host_state / 3.0 + 2.0 / 3.0 * (second_section + host_step * tendency(second_section))
    )
    return (cloud_new, host_new)


def solution(mesh):
    placed = (
        P(("elem", "lev"), None, None),
        P("elem"),
        P("elem", None),
        P(None, "lev", "elem"),
        P(None, "lev", "elem"),
        P("elem"),
        P(),
        P(),
        P(),
    )
    return jax.shard_map(
        shards,
        mesh=mesh,
        in_specs=placed,
        out_specs=(P(("elem", "lev"), None, None), P(None, "lev", "elem")),
        check_vma=False,
    )
```

profile of v0, /device:TPU:230, one launch (start us, length us, event | category | flops | bytes accessed | tf_op | source)
XLA Modules:
  0.0 390.2 jit_solution(18212692638045972472)
XLA Ops:
  1.7 5.4 %collective-permute-start.4 = (f32[1,1,256]{2,1,0:T(1,128)S(1)}, f32[1,1,256]{2,1,0:T(1,128)S(1)}, u32[]{:S(2)}, u32[]{:S(2)}) collective-permute-start(f32[1,1,256]{2,1,0:T(1,128)S(1)} %convolution_bitcast_fusion.4), channel_id=1, source_target_pairs={{0,16},{16,32},{32,48},{48,64},{64,80},{80,96},{96,112},{112,128},... | collective-permute-start | bytes 3080 | tf_op jit(solution)/shard_map/ppermute | solution.py:24
  11.8 2.4 collective-permute-start.1
  18.4 2.1 fusion.136
  24.1 2.1 fusion.134
  26.2 2.1 fusion.133
  28.3 2.1 fusion.135
  30.8 15.3 %all_gather.6 = f32[128,4,64]{0,1,2:T(4,128)S(1)} all-gather(f32[128,4,4]{0,1,2:T(4,128)S(1)} %bitcast.238), channel_id=1, replica_groups=mesh['elem'=32,'lev'=16] {'lev'}, dimensions={2}, use_global_device_ids=true | all-gather | bytes 139264 | tf_op jit(solution)/shard_map/all_gather | solution.py:150
  48.0 68.8 %while.13 = (s32[]{:T(128)}, f32[8,8,4096]{2,1,0:T(8,128)S(1)}, s32[]{:T(128)}, s32[8]{0:T(128)S(1)}, f32[8,8]{1,0:T(8,128)S(1)}, /*index=5*/f32[8,8,64]{2,1,0:T(8,128)S(1)}, s32[]{:T(128)}) while((s32[]{:T(128)}, f32[8,8,4096]{2,1,0:T(8,128)S(1)}, s32[]{:T(128)}, s32[8]{0:T(128)S(1)}, f32[8,8]{1,0:T(8,128)S(1)}, ...), condition=%wide.region_2.3_spmd.clone, body=%wide.region_1.2_spmd.clone.sunk | while | flops 28835848 | bytes 22041208 | solution.py:76
  56.1 3.2 fusion.176
  67.5 3.2 fusion.176
  78.8 3.2 fusion.176
  90.2 3.2 fusion.176
  101.5 3.2 fusion.176
  112.9 3.2 fusion.176
  118.6 2.2 reshape.403
  120.8 2.3 reduce_sum.9
  123.1 17.1 %all_gather.7 = f32[128,8,64]{2,1,0:T(8,128)S(1)} all-gather(f32[8,8,64]{2,1,0:T(8,128)S(1)} %broadcast_multiply_fusion), channel_id=1, replica_groups=mesh['elem'=32,'lev'=16] {'lev'}, dimensions={0}, use_global_device_ids=true | all-gather | bytes 278528 | tf_op jit(solution)/shard_map/all_gather | solution.py:159
  141.9 4.2 %select_select_fusion.3 = s32[512,1]{0,1:T(1,128)S(1)} fusion(s32[]{:T(128)} %bitcast.40, s32[]{:T(128)} %bitcast.41, s32[]{:T(128)} %bitcast.42, s32[]{:T(128)} %bitcast.43, s32[]{:T(128)} %bitcast.44, s32[]{:T(128)} %bitcast.46, s32[]{:T(128)} %bitcast.45), kind=kLoop, calls=%fused_computation.216 | loop fusion | flops 11776 | bytes 2076 | tf_op jit(solution)/shard_map/gather | solution.py:91
  146.1 4.4 %select_select_fusion.2 = s32[512,1]{0,1:T(1,128)S(1)} fusion(s32[]{:T(128)} %bitcast.73, s32[]{:T(128)} %bitcast.74, s32[]{:T(128)} %bitcast.75, s32[]{:T(128)} %bitcast.76, s32[]{:T(128)} %bitcast.77, s32[]{:T(128)} %bitcast.79, s32[]{:T(128)} %bitcast.78), kind=kLoop, calls=%fused_computation.215 | loop fusion | flops 11776 | bytes 2076 | tf_op jit(solution)/shard_map/gather | solution.py:92
  150.4 4.4 %select_select_fusion.1 = s32[512,1]{0,1:T(1,128)S(1)} fusion(s32[]{:T(128)} %bitcast.106, s32[]{:T(128)} %bitcast.107, s32[]{:T(128)} %bitcast.108, s32[]{:T(128)} %bitcast.109, s32[]{:T(128)} %bitcast.110, s32[]{:T(128)} %bitcast.112, s32[]{:T(128)} %bitcast.111), kind=kLoop, calls=%fused_computation.214 | loop fusion | flops 11776 | bytes 2076 | tf_op jit(solution)/shard_map/gather | solution.py:101
  154.9 4.5 %select_select_fusion = s32[512,1]{0,1:T(1,128)S(1)} fusion(s32[]{:T(128)} %bitcast.139, s32[]{:T(128)} %bitcast.140, s32[]{:T(128)} %bitcast.141, s32[]{:T(128)} %bitcast.142, s32[]{:T(128)} %bitcast.143, s32[]{:T(128)} %bitcast.145, s32[]{:T(128)} %bitcast.144), kind=kLoop, calls=%fused_computation.213 | loop fusion | flops 11776 | bytes 2076 | tf_op jit(solution)/shard_map/gather | solution.py:102
  159.3 30.8 %fusion.104 = s32[512]{0:T(512)S(1)} fusion(pred[512]{0:T(512)(128)(4,1)S(1)} %compare_reduce_fusion, pred[512]{0:T(512)(128)(4,1)S(1)} %compare_reduce_fusion.1, pred[512]{0:T(512)(128)(4,1)S(1)} %compare_reduce_fusion.2, pred[512]{0:T(512)(128)(4,1)S(1)} %compare_reduce_fusion.3, pred[512]{0:T(512)(128)(4,1)S(1)} %compare_reduce_fusion.4, ...), kind=kLoop, calls=%fused_computation.204 | loop fusion | flops 53248 | bytes 19144 | tf_op jit(solution)/shard_map/jit(_where)/select_n | solution.py:105
  190.2 31.2 %fusion.94 = s32[512]{0:T(512)S(1)} fusion(pred[512]{0:T(512)(128)(4,1)S(1)} %compare_reduce_fusion, pred[512]{0:T(512)(128)(4,1)S(1)} %compare_reduce_fusion.1, pred[512]{0:T(512)(128)(4,1)S(1)} %compare_reduce_fusion.2, pred[512]{0:T(512)(128)(4,1)S(1)} %compare_reduce_fusion.3, pred[512]{0:T(512)(128)(4,1)S(1)} %compare_reduce_fusion.4, ...), kind=kLoop, calls=%fused_computation.194 | loop fusion | flops 64512 | bytes 19148 | tf_op jit(solution)/shard_map/jit(_where)/select_n | solution.py:97
  223.1 7.2 %collective-permute-start.2 = (f32[4,4,256]{2,1,0:T(4,128)S(1)}, f32[4,4,256]{2,1,0:T(4,128)S(1)}, u32[]{:S(2)}, u32[]{:S(2)}) collective-permute-start(f32[4,4,256]{2,1,0:T(4,128)S(1)} %fusion.37), channel_id=1, source_target_pairs={{0,16},{16,32},{32,48},{48,64},{64,80},{80,96},{96,112},{112,128},... | collective-permute-start | bytes 49160 | tf_op jit(solution)/shard_map/ppermute | solution.py:24
  232.7 6.6 %collective-permute-done.3 = f32[4,4,256]{2,1,0:T(4,128)S(1)} collective-permute-done((f32[4,4,256]{2,1,0:T(4,128)S(1)}, f32[4,4,256]{2,1,0:T(4,128)S(1)}, u32[]{:S(2)}, u32[]{:S(2)}) %collective-permute-start.3) | collective-permute-done | bytes 16416 | tf_op jit(solution)/shard_map/ppermute | solution.py:26
  242.3 2.4 collective-permute-start.7
  245.4 3.1 collective-permute-done.7
  251.4 104.3 %collective-permute-start.9 = (f32[4,4,256]{2,1,0:T(4,128)S(1)}, f32[4,4,256]{2,1,0:T(4,128)S(1)}, u32[]{:S(2)}, u32[]{:S(2)}) collective-permute-start(f32[4,4,256]{2,1,0:T(4,128)S(1)} %fusion.35), channel_id=1, source_target_pairs={{16,0},{32,16},{48,32},{64,48},{80,64},{96,80},{112,96},{128,112},... | collective-permute-start | bytes 49160 | tf_op jit(solution)/shard_map/ppermute | solution.py:26
  360.1 2.4 collective-permute-start.11
  363.2 3.1 collective-permute-done.11
  367.3 12.3 %collective-permute-start.12 = (f32[4,4,256]{2,1,0:T(4,128)S(1)}, f32[4,4,256]{2,1,0:T(4,128)S(1)}, u32[]{:S(2)}, u32[]{:S(2)}) collective-permute-start(f32[4,4,256]{2,1,0:T(4,128)S(1)} %fusion.33), channel_id=1, source_target_pairs={{0,16},{16,32},{32,48},{48,64},{64,80},{80,96},{96,112},{112,128},... | collective-permute-start | bytes 49160 | tf_op jit(solution)/shard_map/ppermute | solution.py:24
  381.5 7.0 %collective-permute-done.13 = f32[4,4,256]{2,1,0:T(4,128)S(1)} collective-permute-done((f32[4,4,256]{2,1,0:T(4,128)S(1)}, f32[4,4,256]{2,1,0:T(4,128)S(1)}, u32[]{:S(2)}, u32[]{:S(2)}) %collective-permute-start.13) | collective-permute-done | bytes 16416 | tf_op jit(solution)/shard_map/ppermute | solution.py:26
  (175 shorter events, 83.7 us)
Async XLA Ops:
  0.6 47.1 %copy-start = (f32[8,4]{0,1:T(4,128)S(1)}, f32[8,4]{0,1:T(4,128)}, u32[]{:S(2)}) copy-start(f32[8,4]{0,1:T(4,128)} %param.20) | copy-start | bytes 388
  0.6 47.3 %copy-start.2 = (f32[8,8,4096]{2,1,0:T(8,128)S(1)}, f32[8,8,4096]{2,1,0:T(8,128)}, u32[]{:S(2)}) copy-start(f32[8,8,4096]{2,1,0:T(8,128)} %param.13) | copy-start | bytes 3145732
  0.7 47.3 %copy-start.6 = (f32[8,8]{1,0:T(8,128)S(1)}, f32[8,8]{1,0:T(8,128)}, u32[]{:S(2)}) copy-start(f32[8,8]{1,0:T(8,128)} %param.19) | copy-start | bytes 772
  1.7 219.8 %collective-permute-start.4 = (f32[1,1,256]{2,1,0:T(1,128)S(1)}, f32[1,1,256]{2,1,0:T(1,128)S(1)}, u32[]{:S(2)}, u32[]{:S(2)}) collective-permute-start(f32[1,1,256]{2,1,0:T(1,128)S(1)} %convolution_bitcast_fusion.4), channel_id=1, source_target_pairs={{0,16},{16,32},{32,48},{48,64},{64,80},{80,96},{96,112},{112,128},... | collective-permute-start | bytes 3080 | tf_op jit(solution)/shard_map/ppermute | solution.py:24
  7.1 214.3 %collective-permute-start.5 = (f32[1,1,256]{2,1,0:T(1,128)S(1)}, f32[1,1,256]{2,1,0:T(1,128)S(1)}, u32[]{:S(2)}, u32[]{:S(2)}) collective-permute-start(f32[1,1,256]{2,1,0:T(1,128)S(1)} %convolution_bitcast_fusion.4), channel_id=1, source_target_pairs={{16,0},{32,16},{48,32},{64,48},{80,64},{96,80},{112,96},{128,112},... | collective-permute-start | bytes 3080 | tf_op jit(solution)/shard_map/ppermute | solution.py:26
  9.9 212.1 %collective-permute-start = (f32[4,1,512]{2,1,0:T(1,128)S(1)}, f32[4,1,512]{2,1,0:T(1,128)S(1)}, u32[]{:S(2)}, u32[]{:S(2)}) collective-permute-start(f32[4,1,512]{2,1,0:T(1,128)S(1)} %get-tuple-element.121), channel_id=1, source_target_pairs={{1,0},{2,1},{3,2},{4,3},{5,4},{6,5},{7,6},{8,7},{9,8},{10,9},{11,1... | collective-permute-start | bytes 24584 | tf_op jit(solution)/shard_map/ppermute | solution.py:26
  11.8 210.2 %collective-permute-start.1 = (f32[4,1,512]{2,1,0:T(1,128)S(1)}, f32[4,1,512]{2,1,0:T(1,128)S(1)}, u32[]{:S(2)}, u32[]{:S(2)}) collective-permute-start(f32[4,1,512]{2,1,0:T(1,128)S(1)} %get-tuple-element.122), channel_id=1, source_target_pairs={{0,1},{1,2},{2,3},{3,4},{4,5},{5,6},{6,7},{7,8},{8,9},{9,10},{10,1... | collective-permute-start | bytes 24584 | tf_op jit(solution)/shard_map/ppermute | solution.py:24
  116.7 4.0 %copy-start.1 = (f32[8,8,4096]{2,1,0:T(8,128)}, f32[8,8,4096]{2,1,0:T(8,128)S(1)}, u32[]{:S(2)}) copy-start(f32[8,8,4096]{2,1,0:T(8,128)S(1)} %get-tuple-element.80) | copy-start | bytes 3145732
  120.7 19.9 %copy-start.9 = (f32[4,8]{1,0:T(4,128)S(1)}, f32[4,8]{1,0:T(4,128)}, u32[]{:S(2)}) copy-start(f32[4,8]{1,0:T(4,128)} %param.21) | copy-start | bytes 388
  120.7 20.4 %copy-start.8 = (f32[2,4,512]{2,1,0:T(4,128)S(1)}, f32[2,4,512]{2,1,0:T(4,128)}, u32[]{:S(2)}) copy-start(f32[2,4,512]{2,1,0:T(4,128)} %param.17) | copy-start | bytes 49156
  120.7 20.4 %copy-start.4 = (f32[512,512,1]{1,0,2:T(8,128)S(1)}, f32[512,512,1]{1,0,2:T(8,128)}, u32[]{:S(2)}) copy-start(f32[512,512,1]{1,0,2:T(8,128)} %constant.378) | copy-start | bytes 3145732
  120.8 20.4 %copy-start.5 = (f32[4,4,512]{2,1,0:T(4,128)S(1)}, f32[4,4,512]{2,1,0:T(4,128)}, u32[]{:S(2)}) copy-start(f32[4,4,512]{2,1,0:T(4,128)} %param.16) | copy-start | bytes 98308
  123.1 98.9 %copy-start.7 = (f32[512]{0:T(512)S(1)}, f32[512]{0:T(512)}, u32[]{:S(2)}) copy-start(f32[512]{0:T(512)} %param.18) | copy-start | bytes 6148
  123.1 99.0 %copy-start.3 = (f32[512,512,1]{1,0,2:T(8,128)S(1)}, f32[512,512,1]{1,0,2:T(8,128)}, u32[]{:S(2)}) copy-start(f32[512,512,1]{1,0,2:T(8,128)} %constant.379) | copy-start | bytes 3145732
  223.1 9.6 %collective-permute-start.2 = (f32[4,4,256]{2,1,0:T(4,128)S(1)}, f32[4,4,256]{2,1,0:T(4,128)S(1)}, u32[]{:S(2)}, u32[]{:S(2)}) collective-permute-start(f32[4,4,256]{2,1,0:T(4,128)S(1)} %fusion.37), channel_id=1, source_target_pairs={{0,16},{16,32},{32,48},{48,64},{64,80},{80,96},{96,112},{112,128},... | collective-permute-start | bytes 49160 | tf_op jit(solution)/shard_map/ppermute | solution.py:24
  230.3 9.0 %collective-permute-start.3 = (f32[4,4,256]{2,1,0:T(4,128)S(1)}, f32[4,4,256]{2,1,0:T(4,128)S(1)}, u32[]{:S(2)}, u32[]{:S(2)}) collective-permute-start(f32[4,4,256]{2,1,0:T(4,128)S(1)} %fusion.37), channel_id=1, source_target_pairs={{16,0},{32,16},{48,32},{64,48},{80,64},{96,80},{112,96},{128,112},... | collective-permute-start | bytes 49160 | tf_op jit(solution)/shard_map/ppermute | solution.py:26
  240.4 5.0 %collective-permute-start.6 = (f32[4,1,512]{2,1,0:T(1,128)S(1)}, f32[4,1,512]{2,1,0:T(1,128)S(1)}, u32[]{:S(2)}, u32[]{:S(2)}) collective-permute-start(f32[4,1,512]{2,1,0:T(1,128)S(1)} %get-tuple-element.119), channel_id=1, source_target_pairs={{1,0},{2,1},{3,2},{4,3},{5,4},{6,5},{7,6},{8,7},{9,8},{10,9},{11,1... | collective-permute-start | bytes 24584 | tf_op jit(solution)/shard_map/ppermute | solution.py:26
  242.3 6.2 %collective-permute-start.7 = (f32[4,1,512]{2,1,0:T(1,128)S(1)}, f32[4,1,512]{2,1,0:T(1,128)S(1)}, u32[]{:S(2)}, u32[]{:S(2)}) collective-permute-start(f32[4,1,512]{2,1,0:T(1,128)S(1)} %get-tuple-element.120), channel_id=1, source_target_pairs={{0,1},{1,2},{2,3},{3,4},{4,5},{5,6},{6,7},{7,8},{8,9},{9,10},{10,1... | collective-permute-start | bytes 24584 | tf_op jit(solution)/shard_map/ppermute | solution.py:24
  249.5 106.2 %collective-permute-start.8 = (f32[4,4,256]{2,1,0:T(4,128)S(1)}, f32[4,4,256]{2,1,0:T(4,128)S(1)}, u32[]{:S(2)}, u32[]{:S(2)}) collective-permute-start(f32[4,4,256]{2,1,0:T(4,128)S(1)} %fusion.35), channel_id=1, source_target_pairs={{0,16},{16,32},{32,48},{48,64},{64,80},{80,96},{96,112},{112,128},... | collective-permute-start | bytes 49160 | tf_op jit(solution)/shard_map/ppermute | solution.py:24
  251.4 105.7 %collective-permute-start.9 = (f32[4,4,256]{2,1,0:T(4,128)S(1)}, f32[4,4,256]{2,1,0:T(4,128)S(1)}, u32[]{:S(2)}, u32[]{:S(2)}) collective-permute-start(f32[4,4,256]{2,1,0:T(4,128)S(1)} %fusion.35), channel_id=1, source_target_pairs={{16,0},{32,16},{48,32},{64,48},{80,64},{96,80},{112,96},{128,112},... | collective-permute-start | bytes 49160 | tf_op jit(solution)/shard_map/ppermute | solution.py:26
  358.2 5.0 %collective-permute-start.10 = (f32[4,1,512]{2,1,0:T(1,128)S(1)}, f32[4,1,512]{2,1,0:T(1,128)S(1)}, u32[]{:S(2)}, u32[]{:S(2)}) collective-permute-start(f32[4,1,512]{2,1,0:T(1,128)S(1)} %get-tuple-element.117), channel_id=1, source_target_pairs={{1,0},{2,1},{3,2},{4,3},{5,4},{6,5},{7,6},{8,7},{9,8},{10,9},{11,1... | collective-permute-start | bytes 24584 | tf_op jit(solution)/shard_map/ppermute | solution.py:26
  360.1 6.2 %collective-permute-start.11 = (f32[4,1,512]{2,1,0:T(1,128)S(1)}, f32[4,1,512]{2,1,0:T(1,128)S(1)}, u32[]{:S(2)}, u32[]{:S(2)}) collective-permute-start(f32[4,1,512]{2,1,0:T(1,128)S(1)} %get-tuple-element.118), channel_id=1, source_target_pairs={{0,1},{1,2},{2,3},{3,4},{4,5},{5,6},{6,7},{7,8},{8,9},{9,10},{10,1... | collective-permute-start | bytes 24584 | tf_op jit(solution)/shard_map/ppermute | solution.py:24
  367.3 14.2 %collective-permute-start.12 = (f32[4,4,256]{2,1,0:T(4,128)S(1)}, f32[4,4,256]{2,1,0:T(4,128)S(1)}, u32[]{:S(2)}, u32[]{:S(2)}) collective-permute-start(f32[4,4,256]{2,1,0:T(4,128)S(1)} %fusion.33), channel_id=1, source_target_pairs={{0,16},{16,32},{32,48},{48,64},{64,80},{80,96},{96,112},{112,128},... | collective-permute-start | bytes 49160 | tf_op jit(solution)/shard_map/ppermute | solution.py:24
  379.5 9.0 %collective-permute-start.13 = (f32[4,4,256]{2,1,0:T(4,128)S(1)}, f32[4,4,256]{2,1,0:T(4,128)S(1)}, u32[]{:S(2)}, u32[]{:S(2)}) collective-permute-start(f32[4,4,256]{2,1,0:T(4,128)S(1)} %fusion.33), channel_id=1, source_target_pairs={{16,0},{32,16},{48,32},{64,48},{80,64},{96,80},{112,96},{128,112},... | collective-permute-start | bytes 49160 | tf_op jit(solution)/shard_map/ppermute | solution.py:26
where the time goes:
time: 393 us; the launch traced here: 390 us
  starting transfers between devices  150 us (38%)
  other arithmetic  93.6 us (24%)
  local copies, waits for them, and re-layouts  56.8 us (14%)
  blocking collectives  32.4 us (8%)
  matrix products  29.9 us (8%)
  waiting for transfers between devices  21.2 us (5%)
  loops' own time  5.2 us (1%)
    ppermute x7, starting transfers between devices, padded_2(): lax.ppermute(head, axis, [((i + 1) % count, i) for i in range(ends)])  116 us
    ppermute x7, starting transfers between devices, padded_2(): lax.ppermute(tail, axis, [(i, (i + 1) % count) for i in range(ends)])  34.1 us
    select_n x1, other arithmetic, edge_tables(): jnp.where(col_of == 0, left_source, jnp.where(col_of == 3, right_source,...  31.2 us
    select_n x1, other arithmetic, edge_tables(): jnp.where(row_of == 0, lower_source, jnp.where(row_of == 3, upper_source,...  30.8 us
    dot_general x6, matrix products, one_step(): jnp.einsum('gf,nfc->ngc', coupling, current, precision=highest)  19 us
    all_gather x1, blocking collectives, shards(): every_change = lax.all_gather(change, 'lev', axis=0, tiled=True)  17.1 us
    all_gather x1, blocking collectives, shards(): every_host = lax.all_gather(host_columns, 'lev', axis=2, tiled=True)  15.3 us
    ppermute x7, waiting for transfers between devices, padded_2(): lax.ppermute(head, axis, [((i + 1) % count, i) for i in range(ends)])  15 us
  transfers between devices with their start and end apart: 14, of which 5 were waited for; matrix products, arithmetic and copies ran while one was open for 44% of the time, Pallas kernels for 0%

commit v1 on v0

--- a/solution.py
+++ b/solution.py
@@ -11,6 +11,12 @@
 host_step = 0.1
 host_mix = 0.2
 highest = lax.Precision.HIGHEST
+
+
+def gather_by_exchange(x, axis, dim):
+    count = lax.axis_size(axis)
+    repeats = [count if d == dim else 1 for d in range(x.ndim)]
+    return lax.all_to_all(jnp.tile(x, repeats), axis, split_axis=dim, concat_axis=dim, tiled=True)
 
 
 def padded_2(cells, sides, width, closed):
@@ -156,7 +162,7 @@
     change = (
         (cloud_new - cloud_state).reshape(own_rows, n_fields, n_levels, cell_width).mean(axis=3)
     )
-    every_change = lax.all_gather(change, "lev", axis=0, tiled=True)
+    every_change = gather_by_exchange(change, "lev", 0)
     level_change = lax.dynamic_slice_in_dim(every_change, lev_at * lev_dev, lev_dev, 2)
     column_tendency = jnp.einsum("vf,nfl->vln", feedback_map, level_change, precision=highest)
     physics = jnp.dot(

time: 393 us -> 378 us (0.962)
  blocking collectives: 32.4 us -> 15.1 us
  local copies, waits for them, and re-layouts: 56.8 us -> 48.4 us
  starting transfers between devices: 150 us -> 158 us
    all_gather x1 -> x0, blocking collectives: 17.1 us -> none  [shards(): every_change = lax.all_gather(change, 'lev', axis=0, tiled=True)]
    all_to_all x0 -> x1, starting transfers between devices: none -> 7.22 us  [gather_by_exchange(): lax.all_to_all(jnp.tile(x, repeats), axis, split_axis=dim, concat_axis=di...]
    gather x4, local copies, waits for them, and re-layouts: 8.41 us -> 2.9 us  [edge_tables(): lower_ids = element_links[:, 2][elem_of] % elem_dev]
  transfers between devices with their start and end apart: 14 -> 15, of which waited for: 5 -> 5; matrix products, arithmetic and copies ran while one was open for 44% -> 44% of each run, Pallas kernels for 0% -> 0%
where the time goes in v1:
time: 378 us; the launch traced here: 375 us
  starting transfers between devices  158 us (42%)
  other arithmetic  95.3 us (25%)
  local copies, waits for them, and re-layouts  48.4 us (13%)
  matrix products  29.9 us (8%)
  waiting for transfers between devices  21.7 us (6%)
  blocking collectives  15.1 us (4%)
  loops' own time  5.2 us (1%)
    ppermute x7, starting transfers between devices, padded_2(): lax.ppermute(head, axis, [((i + 1) % count, i) for i in range(ends)])  118 us
    ppermute x7, starting transfers between devices, padded_2(): lax.ppermute(tail, axis, [(i, (i + 1) % count) for i in range(ends)])  33.2 us
    select_n x1, other arithmetic, edge_tables(): jnp.where(col_of == 0, left_source, jnp.where(col_of == 3, right_source,...  31.2 us
    select_n x1, other arithmetic, edge_tables(): jnp.where(row_of == 0, lower_source, jnp.where(row_of == 3, upper_source,...  31.1 us
    dot_general x6, matrix products, one_step(): jnp.einsum('gf,nfc->ngc', coupling, current, precision=highest)  19 us
    all_gather x1, blocking collectives, shards(): every_host = lax.all_gather(host_columns, 'lev', axis=2, tiled=True)  15.1 us
    ppermute x7, waiting for transfers between devices, padded_2(): lax.ppermute(head, axis, [((i + 1) % count, i) for i in range(ends)])  15 us
    add x6, local copies, waits for them, and re-layouts, one_step(): eastward + westward - 2.0 * current  9.86 us
  transfers between devices with their start and end apart: 15, of which 5 were waited for; matrix products, arithmetic and copies ran while one was open for 44% of the time, Pallas kernels for 0%

profile of v1, /device:TPU:230, one launch (start us, length us, event | category | flops | bytes accessed | tf_op | source)
XLA Modules:
  0.0 375.3 jit_solution(10210923903399305241)
XLA Ops:
  1.7 5.4 %collective-permute-start.4 = (f32[1,1,256]{2,1,0:T(1,128)S(1)}, f32[1,1,256]{2,1,0:T(1,128)S(1)}, u32[]{:S(2)}, u32[]{:S(2)}) collective-permute-start(f32[1,1,256]{2,1,0:T(1,128)S(1)} %convolution_bitcast_fusion.4), channel_id=1, source_target_pairs={{0,16},{16,32},{32,48},{48,64},{64,80},{80,96},{96,112},{112,128},... | collective-permute-start | bytes 3080 | tf_op jit(solution)/shard_map/ppermute | solution.py:30
  10.2 15.1 %all_gather.3 = f32[128,4,64]{0,1,2:T(4,128)S(1)} all-gather(f32[128,4,4]{0,1,2:T(4,128)S(1)} %bitcast.240), channel_id=1, replica_groups=mesh['elem'=32,'lev'=16] {'lev'}, dimensions={2}, use_global_device_ids=true | all-gather | bytes 139264 | tf_op jit(solution)/shard_map/all_gather | solution.py:156
  27.3 68.8 %while.13 = (s32[]{:T(128)}, f32[8,8,4096]{2,1,0:T(8,128)S(1)}, s32[]{:T(128)}, s32[8]{0:T(128)S(1)}, f32[8,8]{1,0:T(8,128)S(1)}, /*index=5*/f32[8,8,64]{2,1,0:T(8,128)S(1)}, s32[]{:T(128)}) while((s32[]{:T(128)}, f32[8,8,4096]{2,1,0:T(8,128)S(1)}, s32[]{:T(128)}, s32[8]{0:T(128)S(1)}, f32[8,8]{1,0:T(8,128)S(1)}, ...), condition=%wide.region_2.3_spmd.clone, body=%wide.region_1.2_spmd.clone.sunk | while | flops 28835848 | bytes 22041208 | solution.py:82
  35.5 3.2 fusion.176
  46.8 3.2 fusion.176
  58.1 3.2 fusion.176
  69.5 3.2 fusion.176
  80.8 3.2 fusion.176
  92.2 3.2 fusion.176
  97.9 2.2 reshape.409
  100.1 2.3 reduce_sum.9
  103.5 7.2 %all-to-all-start = ((f32[16,1,4096]{2,1,0:T(1,128)}), f32[16,1,4096]{2,1,0:T(1,128)S(1)}, u32[]{:S(2)}, u32[]{:S(2)}) async-start(f32[16,1,4096]{2,1,0:T(1,128)} %reshape.1001), calls=%async_computation | async-start | bytes 524288 | tf_op jit(solution)/shard_map/all_to_all | solution.py:19
  110.7 2.2 collective-permute-start
  112.9 2.3 collective-permute-start.1
  122.0 4.4 %select_select_fusion.3 = s32[512,1]{0,1:T(1,128)S(1)} fusion(s32[]{:T(128)} %bitcast.41, s32[]{:T(128)} %bitcast.42, s32[]{:T(128)} %bitcast.43, s32[]{:T(128)} %bitcast.44, s32[]{:T(128)} %bitcast.45, s32[]{:T(128)} %bitcast.47, s32[]{:T(128)} %bitcast.46), kind=kLoop, calls=%fused_computation.216 | loop fusion | flops 11776 | bytes 2076 | tf_op jit(solution)/shard_map/gather | solution.py:97
  126.4 4.5 %select_select_fusion.1 = s32[512,1]{0,1:T(1,128)S(1)} fusion(s32[]{:T(128)} %bitcast.107, s32[]{:T(128)} %bitcast.108, s32[]{:T(128)} %bitcast.109, s32[]{:T(128)} %bitcast.110, s32[]{:T(128)} %bitcast.111, s32[]{:T(128)} %bitcast.113, s32[]{:T(128)} %bitcast.112), kind=kLoop, calls=%fused_computation.214 | loop fusion | flops 11776 | bytes 2076 | tf_op jit(solution)/shard_map/gather | solution.py:107
  130.9 4.4 %select_select_fusion = s32[512,1]{0,1:T(1,128)S(1)} fusion(s32[]{:T(128)} %bitcast.140, s32[]{:T(128)} %bitcast.141, s32[]{:T(128)} %bitcast.142, s32[]{:T(128)} %bitcast.143, s32[]{:T(128)} %bitcast.144, s32[]{:T(128)} %bitcast.146, s32[]{:T(128)} %bitcast.145), kind=kLoop, calls=%fused_computation.213 | loop fusion | flops 11776 | bytes 2076 | tf_op jit(solution)/shard_map/gather | solution.py:108
  135.3 31.1 %fusion.104 = s32[512]{0:T(512)S(1)} fusion(pred[512]{0:T(512)(128)(4,1)S(1)} %compare_reduce_fusion, pred[512]{0:T(512)(128)(4,1)S(1)} %compare_reduce_fusion.1, pred[512]{0:T(512)(128)(4,1)S(1)} %compare_reduce_fusion.2, pred[512]{0:T(512)(128)(4,1)S(1)} %compare_reduce_fusion.3, pred[512]{0:T(512)(128)(4,1)S(1)} %compare_reduce_fusion.4, ...), kind=kLoop, calls=%fused_computation.204 | loop fusion | flops 53248 | bytes 19144 | tf_op jit(solution)/shard_map/jit(_where)/select_n | solution.py:111
  166.4 4.4 %select_select_fusion.2 = s32[512,1]{0,1:T(1,128)S(1)} fusion(s32[]{:T(128)} %bitcast.74, s32[]{:T(128)} %bitcast.75, s32[]{:T(128)} %bitcast.76, s32[]{:T(128)} %bitcast.77, s32[]{:T(128)} %bitcast.78, s32[]{:T(128)} %bitcast.80, s32[]{:T(128)} %bitcast.79), kind=kLoop, calls=%fused_computation.215 | loop fusion | flops 11776 | bytes 2076 | tf_op jit(solution)/shard_map/gather | solution.py:98
  170.8 31.2 %fusion.94 = s32[512]{0:T(512)S(1)} fusion(pred[512]{0:T(512)(128)(4,1)S(1)} %compare_reduce_fusion, pred[512]{0:T(512)(128)(4,1)S(1)} %compare_reduce_fusion.1, pred[512]{0:T(512)(128)(4,1)S(1)} %compare_reduce_fusion.2, pred[512]{0:T(512)(128)(4,1)S(1)} %compare_reduce_fusion.3, pred[512]{0:T(512)(128)(4,1)S(1)} %compare_reduce_fusion.4, ...), kind=kLoop, calls=%fused_computation.194 | loop fusion | flops 64512 | bytes 19148 | tf_op jit(solution)/shard_map/jit(_where)/select_n | solution.py:103
  206.6 7.2 %collective-permute-start.2 = (f32[4,4,256]{2,1,0:T(4,128)S(1)}, f32[4,4,256]{2,1,0:T(4,128)S(1)}, u32[]{:S(2)}, u32[]{:S(2)}) collective-permute-start(f32[4,4,256]{2,1,0:T(4,128)S(1)} %fusion.37), channel_id=1, source_target_pairs={{0,16},{16,32},{32,48},{48,64},{64,80},{80,96},{96,112},{112,128},... | collective-permute-start | bytes 49160 | tf_op jit(solution)/shard_map/ppermute | solution.py:30
  213.9 1.9 collective-permute-start.3
  216.2 6.6 %collective-permute-done.3 = f32[4,4,256]{2,1,0:T(4,128)S(1)} collective-permute-done((f32[4,4,256]{2,1,0:T(4,128)S(1)}, f32[4,4,256]{2,1,0:T(4,128)S(1)}, u32[]{:S(2)}, u32[]{:S(2)}) %collective-permute-start.3) | collective-permute-done | bytes 16416 | tf_op jit(solution)/shard_map/ppermute | solution.py:32
  224.0 3.1 collective-permute-start.6
  227.1 1.9 collective-permute-start.7
  229.7 3.6 collective-permute-done.7
  234.3 1.9 collective-permute-start.8
  236.2 104.8 %collective-permute-start.9 = (f32[4,4,256]{2,1,0:T(4,128)S(1)}, f32[4,4,256]{2,1,0:T(4,128)S(1)}, u32[]{:S(2)}, u32[]{:S(2)}) collective-permute-start(f32[4,4,256]{2,1,0:T(4,128)S(1)} %fusion.35), channel_id=1, source_target_pairs={{16,0},{32,16},{48,32},{64,48},{80,64},{96,80},{112,96},{128,112},... | collective-permute-start | bytes 49160 | tf_op jit(solution)/shard_map/ppermute | solution.py:32
  345.5 2.4 collective-permute-start.11
  348.6 3.1 collective-permute-done.11
  352.6 12.0 %collective-permute-start.12 = (f32[4,4,256]{2,1,0:T(4,128)S(1)}, f32[4,4,256]{2,1,0:T(4,128)S(1)}, u32[]{:S(2)}, u32[]{:S(2)}) collective-permute-start(f32[4,4,256]{2,1,0:T(4,128)S(1)} %fusion.33), channel_id=1, source_target_pairs={{0,16},{16,32},{32,48},{48,64},{64,80},{80,96},{96,112},{112,128},... | collective-permute-start | bytes 49160 | tf_op jit(solution)/shard_map/ppermute | solution.py:30
  366.6 7.0 %collective-permute-done.13 = f32[4,4,256]{2,1,0:T(4,128)S(1)} collective-permute-done((f32[4,4,256]{2,1,0:T(4,128)S(1)}, f32[4,4,256]{2,1,0:T(4,128)S(1)}, u32[]{:S(2)}, u32[]{:S(2)}) %collective-permute-start.13) | collective-permute-done | bytes 16416 | tf_op jit(solution)/shard_map/ppermute | solution.py:32
  (183 shorter events, 77.3 us)
Async XLA Ops:
  0.6 26.4 %copy-start = (f32[8,4]{0,1:T(4,128)S(1)}, f32[8,4]{0,1:T(4,128)}, u32[]{:S(2)}) copy-start(f32[8,4]{0,1:T(4,128)} %param.20) | copy-start | bytes 388
  0.6 26.6 %copy-start.2 = (f32[8,8,4096]{2,1,0:T(8,128)S(1)}, f32[8,8,4096]{2,1,0:T(8,128)}, u32[]{:S(2)}) copy-start(f32[8,8,4096]{2,1,0:T(8,128)} %param.13) | copy-start | bytes 3145732
  0.7 26.6 %copy-start.7 = (f32[8,8]{1,0:T(8,128)S(1)}, f32[8,8]{1,0:T(8,128)}, u32[]{:S(2)}) copy-start(f32[8,8]{1,0:T(8,128)} %param.19) | copy-start | bytes 772
  1.7 200.3 %collective-permute-start.4 = (f32[1,1,256]{2,1,0:T(1,128)S(1)}, f32[1,1,256]{2,1,0:T(1,128)S(1)}, u32[]{:S(2)}, u32[]{:S(2)}) collective-permute-start(f32[1,1,256]{2,1,0:T(1,128)S(1)} %convolution_bitcast_fusion.4), channel_id=1, source_target_pairs={{0,16},{16,32},{32,48},{48,64},{64,80},{80,96},{96,112},{112,128},... | collective-permute-start | bytes 3080 | tf_op jit(solution)/shard_map/ppermute | solution.py:30
  7.1 194.9 %collective-permute-start.5 = (f32[1,1,256]{2,1,0:T(1,128)S(1)}, f32[1,1,256]{2,1,0:T(1,128)S(1)}, u32[]{:S(2)}, u32[]{:S(2)}) collective-permute-start(f32[1,1,256]{2,1,0:T(1,128)S(1)} %convolution_bitcast_fusion.4), channel_id=1, source_target_pairs={{16,0},{32,16},{48,32},{64,48},{80,64},{96,80},{112,96},{128,112},... | collective-permute-start | bytes 3080 | tf_op jit(solution)/shard_map/ppermute | solution.py:32
  96.0 4.0 %copy-start.1 = (f32[8,8,4096]{2,1,0:T(8,128)}, f32[8,8,4096]{2,1,0:T(8,128)S(1)}, u32[]{:S(2)}) copy-start(f32[8,8,4096]{2,1,0:T(8,128)S(1)} %get-tuple-element.80) | copy-start | bytes 3145732
  100.0 10.6 %copy-start.6 = (f32[4,4,512]{2,1,0:T(4,128)S(1)}, f32[4,4,512]{2,1,0:T(4,128)}, u32[]{:S(2)}) copy-start(f32[4,4,512]{2,1,0:T(4,128)} %param.16) | copy-start | bytes 98308
  100.0 15.2 %copy-start.5 = (s32[32,4]{0,1:T(4,128)S(1)}, s32[32,4]{0,1:T(4,128)}, u32[]{:S(2)}) copy-start(s32[32,4]{0,1:T(4,128)} %param.15) | copy-start | bytes 1540
  100.0 21.1 %copy-start.9 = (f32[2,4,512]{2,1,0:T(4,128)S(1)}, f32[2,4,512]{2,1,0:T(4,128)}, u32[]{:S(2)}) copy-start(f32[2,4,512]{2,1,0:T(4,128)} %param.17) | copy-start | bytes 49156
  100.1 21.2 %copy-start.4 = (f32[512,512,1]{1,0,2:T(8,128)S(1)}, f32[512,512,1]{1,0,2:T(8,128)}, u32[]{:S(2)}) copy-start(f32[512,512,1]{1,0,2:T(8,128)} %constant.378) | copy-start | bytes 3145732
  102.4 100.2 %copy-start.8 = (f32[512]{0:T(512)S(1)}, f32[512]{0:T(512)}, u32[]{:S(2)}) copy-start(f32[512]{0:T(512)} %param.18) | copy-start | bytes 6148
  103.5 99.2 %all-to-all-start = ((f32[16,1,4096]{2,1,0:T(1,128)}), f32[16,1,4096]{2,1,0:T(1,128)S(1)}, u32[]{:S(2)}, u32[]{:S(2)}) async-start(f32[16,1,4096]{2,1,0:T(1,128)} %reshape.1001), calls=%async_computation | async-start | bytes 524288 | tf_op jit(solution)/shard_map/all_to_all | solution.py:19
  110.7 94.8 %collective-permute-start = (f32[4,1,512]{2,1,0:T(1,128)S(1)}, f32[4,1,512]{2,1,0:T(1,128)S(1)}, u32[]{:S(2)}, u32[]{:S(2)}) collective-permute-start(f32[4,1,512]{2,1,0:T(1,128)S(1)} %get-tuple-element.121), channel_id=1, source_target_pairs={{1,0},{2,1},{3,2},{4,3},{5,4},{6,5},{7,6},{8,7},{9,8},{10,9},{11,1... | collective-permute-start | bytes 24584 | tf_op jit(solution)/shard_map/ppermute | solution.py:32
  112.9 92.7 %collective-permute-start.1 = (f32[4,1,512]{2,1,0:T(1,128)S(1)}, f32[4,1,512]{2,1,0:T(1,128)S(1)}, u32[]{:S(2)}, u32[]{:S(2)}) collective-permute-start(f32[4,1,512]{2,1,0:T(1,128)S(1)} %get-tuple-element.122), channel_id=1, source_target_pairs={{0,1},{1,2},{2,3},{3,4},{4,5},{5,6},{6,7},{7,8},{8,9},{9,10},{10,1... | collective-permute-start | bytes 24584 | tf_op jit(solution)/shard_map/ppermute | solution.py:30
  122.0 83.1 %copy-start.10 = (f32[4,8]{1,0:T(4,128)S(1)}, f32[4,8]{1,0:T(4,128)}, u32[]{:S(2)}) copy-start(f32[4,8]{1,0:T(4,128)} %param.21) | copy-start | bytes 388
  122.0 83.6 %copy-start.3 = (f32[512,512,1]{1,0,2:T(8,128)S(1)}, f32[512,512,1]{1,0,2:T(8,128)}, u32[]{:S(2)}) copy-start(f32[512,512,1]{1,0,2:T(8,128)} %constant.379) | copy-start | bytes 3145732
  206.6 9.6 %collective-permute-start.2 = (f32[4,4,256]{2,1,0:T(4,128)S(1)}, f32[4,4,256]{2,1,0:T(4,128)S(1)}, u32[]{:S(2)}, u32[]{:S(2)}) collective-permute-start(f32[4,4,256]{2,1,0:T(4,128)S(1)} %fusion.37), channel_id=1, source_target_pairs={{0,16},{16,32},{32,48},{48,64},{64,80},{80,96},{96,112},{112,128},... | collective-permute-start | bytes 49160 | tf_op jit(solution)/shard_map/ppermute | solution.py:30
  213.9 9.0 %collective-permute-start.3 = (f32[4,4,256]{2,1,0:T(4,128)S(1)}, f32[4,4,256]{2,1,0:T(4,128)S(1)}, u32[]{:S(2)}, u32[]{:S(2)}) collective-permute-start(f32[4,4,256]{2,1,0:T(4,128)S(1)} %fusion.37), channel_id=1, source_target_pairs={{16,0},{32,16},{48,32},{64,48},{80,64},{96,80},{112,96},{128,112},... | collective-permute-start | bytes 49160 | tf_op jit(solution)/shard_map/ppermute | solution.py:32
  224.0 5.7 %collective-permute-start.6 = (f32[4,1,512]{2,1,0:T(1,128)S(1)}, f32[4,1,512]{2,1,0:T(1,128)S(1)}, u32[]{:S(2)}, u32[]{:S(2)}) collective-permute-start(f32[4,1,512]{2,1,0:T(1,128)S(1)} %get-tuple-element.119), channel_id=1, source_target_pairs={{1,0},{2,1},{3,2},{4,3},{5,4},{6,5},{7,6},{8,7},{9,8},{10,9},{11,1... | collective-permute-start | bytes 24584 | tf_op jit(solution)/shard_map/ppermute | solution.py:32
  227.1 6.2 %collective-permute-start.7 = (f32[4,1,512]{2,1,0:T(1,128)S(1)}, f32[4,1,512]{2,1,0:T(1,128)S(1)}, u32[]{:S(2)}, u32[]{:S(2)}) collective-permute-start(f32[4,1,512]{2,1,0:T(1,128)S(1)} %get-tuple-element.120), channel_id=1, source_target_pairs={{0,1},{1,2},{2,3},{3,4},{4,5},{5,6},{6,7},{7,8},{8,9},{9,10},{10,1... | collective-permute-start | bytes 24584 | tf_op jit(solution)/shard_map/ppermute | solution.py:30
  234.3 106.8 %collective-permute-start.8 = (f32[4,4,256]{2,1,0:T(4,128)S(1)}, f32[4,4,256]{2,1,0:T(4,128)S(1)}, u32[]{:S(2)}, u32[]{:S(2)}) collective-permute-start(f32[4,4,256]{2,1,0:T(4,128)S(1)} %fusion.35), channel_id=1, source_target_pairs={{0,16},{16,32},{32,48},{48,64},{64,80},{80,96},{96,112},{112,128},... | collective-permute-start | bytes 49160 | tf_op jit(solution)/shard_map/ppermute | solution.py:30
  236.2 106.3 %collective-permute-start.9 = (f32[4,4,256]{2,1,0:T(4,128)S(1)}, f32[4,4,256]{2,1,0:T(4,128)S(1)}, u32[]{:S(2)}, u32[]{:S(2)}) collective-permute-start(f32[4,4,256]{2,1,0:T(4,128)S(1)} %fusion.35), channel_id=1, source_target_pairs={{16,0},{32,16},{48,32},{64,48},{80,64},{96,80},{112,96},{128,112},... | collective-permute-start | bytes 49160 | tf_op jit(solution)/shard_map/ppermute | solution.py:32
  343.6 5.0 %collective-permute-start.10 = (f32[4,1,512]{2,1,0:T(1,128)S(1)}, f32[4,1,512]{2,1,0:T(1,128)S(1)}, u32[]{:S(2)}, u32[]{:S(2)}) collective-permute-start(f32[4,1,512]{2,1,0:T(1,128)S(1)} %get-tuple-element.117), channel_id=1, source_target_pairs={{1,0},{2,1},{3,2},{4,3},{5,4},{6,5},{7,6},{8,7},{9,8},{10,9},{11,1... | collective-permute-start | bytes 24584 | tf_op jit(solution)/shard_map/ppermute | solution.py:32
  345.5 6.2 %collective-permute-start.11 = (f32[4,1,512]{2,1,0:T(1,128)S(1)}, f32[4,1,512]{2,1,0:T(1,128)S(1)}, u32[]{:S(2)}, u32[]{:S(2)}) collective-permute-start(f32[4,1,512]{2,1,0:T(1,128)S(1)} %get-tuple-element.118), channel_id=1, source_target_pairs={{0,1},{1,2},{2,3},{3,4},{4,5},{5,6},{6,7},{7,8},{8,9},{9,10},{10,1... | collective-permute-start | bytes 24584 | tf_op jit(solution)/shard_map/ppermute | solution.py:30
  352.6 13.9 %collective-permute-start.12 = (f32[4,4,256]{2,1,0:T(4,128)S(1)}, f32[4,4,256]{2,1,0:T(4,128)S(1)}, u32[]{:S(2)}, u32[]{:S(2)}) collective-permute-start(f32[4,4,256]{2,1,0:T(4,128)S(1)} %fusion.33), channel_id=1, source_target_pairs={{0,16},{16,32},{32,48},{48,64},{64,80},{80,96},{96,112},{112,128},... | collective-permute-start | bytes 49160 | tf_op jit(solution)/shard_map/ppermute | solution.py:30
  364.6 9.0 %collective-permute-start.13 = (f32[4,4,256]{2,1,0:T(4,128)S(1)}, f32[4,4,256]{2,1,0:T(4,128)S(1)}, u32[]{:S(2)}, u32[]{:S(2)}) collective-permute-start(f32[4,4,256]{2,1,0:T(4,128)S(1)} %fusion.33), channel_id=1, source_target_pairs={{16,0},{32,16},{48,32},{64,48},{80,64},{96,80},{112,96},{128,112},... | collective-permute-start | bytes 49160 | tf_op jit(solution)/shard_map/ppermute | solution.py:32
